TPU v7x, 32 devices: a whole 2x2x4 slice. The times are simulated.
32 devices in a mesh: section: 2 (over x), dp: 16 (over z, y, core).
Axes of the slice: x: 2, y: 2, z: 4, core: 2. Of those that a mesh axis runs over, the one named last changes fastest.
Arguments:
- inputs: bfloat16 [4, 2048, 1536], P(None, 'dp'), may hold values from -6 to 6
- out_grad: bfloat16 [4, 2048, 1536], P(None, 'dp'), may hold values from -0.125 to 0.125
- guide_bin: int32 [4, 1], replicated, may hold values from 0 to 31
- time_step: int32 [4, 1], replicated, may hold values from 0 to 999
- guide_table: bfloat16 [32, 4608], replicated, may hold values from -3 to 3
- section_table: float32 [2, 3, 1536], P('section'), may hold values from -3 to 3
- value_weight: bfloat16 [2, 1536, 1536], P('section'), may hold values from -0.15625 to 0.15625
- proj_weight: bfloat16 [2, 1536, 1536], P('section'), may hold values from -0.15625 to 0.15625
Outputs:
- value_grad: float32 [2, 1536, 1536], P('section', 'dp')
- proj_grad: float32 [2, 1536, 1536], P('section', 'dp')
- table_grad: float32 [2, 3, 1536], P('section', None, 'dp')
All inputs are finite; a program needn't handle non-finite values.
Results may differ from a plain program's by a relative error of at most 0.017.
Values may be sent and summed in bfloat16 or wider, within the bound.
A program may use at most 128 MiB of HBM per device.

v0:
```python
import functools
import math

import jax
import jax.numpy as jnp
from jax import lax
from jax.experimental import pallas as pl
from jax.experimental.pallas import tpu as pltpu
from jax.sharding import PartitionSpec as P

NORM_FLOOR = 0.1


def shifted(value, axis, steps):
    count = lax.axis_size(axis)
    leading, last = (max(0, -steps), min(count, count - steps))
    return lax.ppermute(value, axis, [(source, source + steps) for source in range(leading, last)])


def normalize(hidden):
    centre = jnp.mean(hidden, axis=-1, keepdims=True)
    centred = hidden - centre
    spread = jnp.mean(centred * centred, axis=-1, keepdims=True)
    inverse = lax.rsqrt(spread + NORM_FLOOR)
    return (centred * inverse, inverse)


def conditions(guide_bin, time_step, guide_table):
    total = guide_table.shape[1]
    half = total // 2
    frequency = jnp.exp(-math.log(10000.0) * jnp.arange(half, dtype=jnp.float32) / half)
    angle = time_step.astype(jnp.float32)[..., None] * frequency
    waves = jnp.concatenate([jnp.sin(angle), jnp.cos(angle)], axis=-1)
    bin_count = guide_table.shape[0]
    onehot = (guide_bin[..., None] == jnp.arange(bin_count, dtype=jnp.int32)).astype(jnp.float32)
    picked = jnp.einsum(
        "msb,bw->msw", onehot, guide_table.astype(jnp.float32), precision=lax.Precision.HIGHEST
    )
    return picked + 0.5 * waves


def contract_rows(left, right):
    return lax.dot_general(
        left, right, (((0,), (0,)), ((), ())), preferred_element_type=jnp.float32
    )


def forward_block(block_in, modulation, value_weight, proj_weight):
    width = block_in.shape[1]
    hidden = block_in.astype(jnp.float32)
    normed, inverse = normalize(hidden)
    shift = modulation[:, :width]
    scale = modulation[:, width : 2 * width]
    gate = modulation[:, 2 * width :]
    modulated = (normed * (1.0 + scale) + shift).astype(jnp.bfloat16)
    values = jnp.dot(modulated, value_weight, preferred_element_type=jnp.float32).astype(
        jnp.bfloat16
    )
    projected = jnp.dot(values, proj_weight, preferred_element_type=jnp.float32)
    block_out = (hidden + gate * projected).astype(jnp.bfloat16)
    return (block_out, modulated, values, projected)


def backward_block(block_in, projected, upstream, modulation, value_weight, proj_weight):
    width = block_in.shape[1]
    hidden = block_in.astype(jnp.float32)
    normed, inverse = normalize(hidden)
    scale = modulation[:, width : 2 * width]
    gate = modulation[:, 2 * width :]
    grad_up = upstream.astype(jnp.float32)
    grad_proj = (gate * grad_up).astype(jnp.bfloat16)
    grad_values = lax.dot_general(
        grad_proj, proj_weight, (((1,), (1,)), ((), ())), preferred_element_type=jnp.float32
    ).astype(jnp.bfloat16)
    grad_mod = lax.dot_general(
        grad_values, value_weight, (((1,), (1,)), ((), ())), preferred_element_type=jnp.float32
    )
    part_table = jnp.stack(
        [
            jnp.sum(grad_mod, axis=0),
            jnp.sum(grad_mod * normed, axis=0),
            jnp.sum(grad_up * projected, axis=0),
        ]
    )
    grad_norm = grad_mod * (1.0 + scale)
    centre_grad = jnp.mean(grad_norm, axis=-1, keepdims=True)
    cross = jnp.mean(grad_norm * normed, axis=-1, keepdims=True)
    grad_in = grad_up + inverse * (grad_norm - centre_grad - normed * cross)
    return (grad_in.astype(jnp.bfloat16), grad_values, grad_proj, part_table)


def per_device_scan(
    inputs, out_grad, guide_bin, time_step, guide_table, section_table, value_weight, proj_weight
):
    sections = lax.axis_size("section")
    section_id = lax.axis_index("section")
    position = lax.axis_index("dp")
    group_size = lax.axis_size("dp")
    tok_dev = inputs.shape[1]
    width = inputs.shape[2]
    value_width = value_weight.shape[2]
    batches = inputs.shape[0]
    samples = guide_bin.shape[1]
    tokens = tok_dev * group_size
    rows_per = tokens // samples
    parts = 1
    unit_rows = tok_dev // parts
    units = batches * parts
    condition = conditions(guide_bin, time_step, guide_table)
    weights_value = value_weight[0]
    weights_proj = proj_weight[0]
    section_row = section_table[0].reshape(-1)
    sample_ids = jnp.arange(samples, dtype=jnp.int32)

    def unit_modulation(unit_id):
        batch_id = unit_id // parts
        piece_id = unit_id % parts
        chosen = lax.dynamic_index_in_dim(condition, batch_id, 0, keepdims=False)
        global_rows = (
            position * tok_dev + piece_id * unit_rows + jnp.arange(unit_rows, dtype=jnp.int32)
        )
        owner = global_rows // rows_per
        onehot = (owner[:, None] == sample_ids[None, :]).astype(jnp.float32)
        picked = jnp.dot(
            onehot, chosen, precision=lax.Precision.HIGHEST, preferred_element_type=jnp.float32
        )
        return picked + section_row

    slots = units + 1
    keep_in = jnp.zeros((slots, unit_rows, width), jnp.bfloat16)
    keep_mod = jnp.zeros((slots, unit_rows, width), jnp.bfloat16)
    keep_val = jnp.zeros((slots, unit_rows, value_width), jnp.bfloat16)
    keep_proj = jnp.zeros((slots, unit_rows, width), jnp.float32)
    arriving = jnp.zeros((unit_rows, width), jnp.bfloat16)

    def forward_tick(carry, tick_id):
        incoming, saved_in, saved_mod, saved_val, saved_proj = carry
        unit_id = tick_id - section_id
        valid = (unit_id >= 0) & (unit_id < units)
        clipped = jnp.clip(unit_id, 0, units - 1)
        first = lax.dynamic_index_in_dim(inputs, clipped, 0, keepdims=False)
        block_in = jnp.where(section_id == 0, first, incoming)

        def forward_active(operand):
            return forward_block(operand, unit_modulation(clipped), weights_value, weights_proj)

        def forward_resting(operand):
            return (
                jnp.zeros_like(operand),
                jnp.zeros_like(operand),
                jnp.zeros((unit_rows, value_width), jnp.bfloat16),
                jnp.zeros((unit_rows, width), jnp.float32),
            )

        block_out, modulated, values, projected = lax.cond(
            valid, forward_active, forward_resting, block_in
        )
        slot_id = jnp.where(valid, unit_id, units)
        saved_in = lax.dynamic_update_index_in_dim(saved_in, block_in, slot_id, 0)
        saved_mod = lax.dynamic_update_index_in_dim(saved_mod, modulated, slot_id, 0)
        saved_val = lax.dynamic_update_index_in_dim(saved_val, values, slot_id, 0)
        saved_proj = lax.dynamic_update_index_in_dim(saved_proj, projected, slot_id, 0)
        sent = shifted(block_out, "section", 1)
        return ((sent, saved_in, saved_mod, saved_val, saved_proj), None)

    ticks = jnp.arange(units + sections - 1, dtype=jnp.int32)
    carry, unused = lax.scan(
        forward_tick, (arriving, keep_in, keep_mod, keep_val, keep_proj), ticks
    )
    arriving, keep_in, keep_mod, keep_val, keep_proj = carry
    store = jnp.zeros((slots, unit_rows, value_width), jnp.bfloat16)
    extra_zero = jnp.zeros((unit_rows, value_width), jnp.bfloat16)
    keep_grad = jnp.zeros((slots, unit_rows, width), jnp.bfloat16)
    proj_sum = jnp.zeros((value_width, width), jnp.float32)
    table_sum = jnp.zeros((3, width), jnp.float32)

    def backward_tick(carry, tick_id):
        incoming, store_now, grads_now, proj_now, table_now = carry
        unit_id = tick_id - (sections - 1 - section_id)
        valid = (unit_id >= 0) & (unit_id < units)
        clipped = jnp.clip(unit_id, 0, units - 1)
        last = lax.dynamic_index_in_dim(out_grad, clipped, 0, keepdims=False)
        upstream = jnp.where(section_id == sections - 1, last, incoming)
        block_in = lax.dynamic_index_in_dim(keep_in, clipped, 0, keepdims=False)
        modulated = lax.dynamic_index_in_dim(keep_mod, clipped, 0, keepdims=False)
        values = lax.dynamic_index_in_dim(keep_val, clipped, 0, keepdims=False)
        projected = lax.dynamic_index_in_dim(keep_proj, clipped, 0, keepdims=False)

        def backward_active(operand):
            grad_in, grad_values, grad_proj, part_table = backward_block(
                block_in, projected, operand, unit_modulation(clipped), weights_value, weights_proj
            )
            part_proj = jnp.zeros((value_width, width), jnp.float32)
            return (grad_in, grad_values, grad_proj, part_proj, part_table)

        def backward_resting(operand):
            return (
                jnp.zeros_like(operand),
                extra_zero,
                jnp.zeros((unit_rows, width), jnp.bfloat16),
                jnp.zeros((value_width, width), jnp.float32),
                jnp.zeros((3, width), jnp.float32),
            )

        grad_in, extra, grad_proj, part_proj, part_table = lax.cond(
            valid, backward_active, backward_resting, upstream
        )
        slot_id = jnp.where(valid, unit_id, units)
        store_now = lax.dynamic_update_index_in_dim(store_now, extra, slot_id, 0)
        grads_now = lax.dynamic_update_index_in_dim(grads_now, grad_proj, slot_id, 0)
        sent = shifted(grad_in, "section", -1)
        return ((sent, store_now, grads_now, proj_now + part_proj, table_now + part_table), None)

    carry, unused = lax.scan(
        backward_tick, (arriving, store, keep_grad, proj_sum, table_sum), ticks
    )
    arriving, store, keep_grad, proj_sum, table_sum = carry
    mod_rows = keep_mod[:units].reshape(units * unit_rows, width)
    grad_rows = store[:units].reshape(units * unit_rows, value_width)
    columns = mod_rows
    value_part = lax.psum_scatter(
        contract_rows(columns, grad_rows), "dp", scatter_dimension=0, tiled=True
    )
    val_rows = keep_val[:units].reshape(units * unit_rows, value_width)
    upper_rows = keep_grad[:units].reshape(units * unit_rows, width)
    columns = val_rows
    proj_part = lax.psum_scatter(
        contract_rows(columns, upper_rows), "dp", scatter_dimension=0, tiled=True
    )
    table_part = lax.psum_scatter(table_sum, "dp", scatter_dimension=1, tiled=True)
    return (value_part[None], proj_part[None], table_part[None])


MESH = pl.DeviceIdType.MESH


def scatter_kernel(far, value_ref, proj_ref, table_ref, value_out, proj_out, table_out,
                   core_in, own, side_out, side_in, far_out, far_in, table_in,
                   core_send, core_recv, side_send, side_recv, far_send, far_recv,
                   table_send, table_recv):
    group = 4 * far
    me = lax.axis_index("dp")
    core, side, place = me % 2, (me // 2) % 2, me // 4
    barrier = pltpu.get_barrier_semaphore()
    for step in range(1, group):
        pl.semaphore_signal(
            barrier, inc=1, device_id={"dp": (me + step) % group}, device_id_type=MESH
        )
    pl.semaphore_wait(barrier, group - 1)

    matrices = (proj_ref, value_ref)
    offsets = [(far // 2 + step) % far for step in range(far)]
    offsets = [offset for offset in offsets if offset] + [0]
    pieces = [(matrix, slot) for matrix in range(2) for slot in range(far)]

    def row(slot, which_side, which_core):
        return (((place + offsets[slot]) % far) * 2 + which_side) * 2 + which_core

    core_copies = {}
    for turn in range(2):
        for index, (matrix, slot) in enumerate(pieces):
            which = (1 - side) if turn == 0 else side
            copy = pltpu.make_async_remote_copy(
                src_ref=matrices[matrix].at[row(slot, which, 1 - core)],
                dst_ref=core_in.at[turn, index],
                send_sem=core_send.at[turn, index],
                recv_sem=core_recv.at[turn, index],
                device_id={"dp": me - core + (1 - core)},
                device_id_type=MESH,
            )
            copy.start()
            core_copies[turn, index] = copy
    table_copies = []
    for step in range(1, group):
        copy = pltpu.make_async_remote_copy(
            src_ref=table_ref.at[(me + step) % group],
            dst_ref=table_in.at[step - 1],
            send_sem=table_send.at[step - 1],
            recv_sem=table_recv.at[step - 1],
            device_id={"dp": (me + step) % group},
            device_id_type=MESH,
        )
        copy.start()
        table_copies.append(copy)

    side_copies = []
    for index, (matrix, slot) in enumerate(pieces):
        core_copies[0, index].wait_recv()
        mine = matrices[matrix][row(slot, 1 - side, core)].astype(jnp.float32)
        side_out[index] = (mine + core_in[0, index].astype(jnp.float32)).astype(jnp.bfloat16)
        copy = pltpu.make_async_remote_copy(
            src_ref=side_out.at[index],
            dst_ref=side_in.at[index],
            send_sem=side_send.at[index],
            recv_sem=side_recv.at[index],
            device_id={"dp": me + 2 - 4 * side},
            device_id_type=MESH,
        )
        copy.start()
        side_copies.append(copy)
    far_copies = {}
    for index, (matrix, slot) in enumerate(pieces):
        core_copies[1, index].wait_recv()
        mine = matrices[matrix][row(slot, side, core)].astype(jnp.float32)
        mine = mine + core_in[1, index].astype(jnp.float32)
        side_copies[index].wait_recv()
        mine = mine + side_in[index].astype(jnp.float32)
        if offsets[slot] == 0:
            own[matrix] = mine
        else:
            far_out[index] = mine.astype(jnp.bfloat16)
            copy = pltpu.make_async_remote_copy(
                src_ref=far_out.at[index],
                dst_ref=far_in.at[index],
                send_sem=far_send.at[index],
                recv_sem=far_recv.at[index],
                device_id={"dp": (me + 4 * offsets[slot]) % group},
                device_id_type=MESH,
            )
            copy.start()
            far_copies[index] = copy
    total = table_ref[me]
    for step in range(1, group):
        table_copies[step - 1].wait_recv()
        total = total + table_in[step - 1]
    table_out[...] = total
    for matrix, out in enumerate((proj_out, value_out)):
        result = own[matrix]
        for index, (which, slot) in enumerate(pieces):
            if which == matrix and index in far_copies:
                far_copies[index].wait_recv()
                result = result + far_in[index].astype(jnp.float32)
        out[...] = result
    for copy in list(core_copies.values()) + table_copies + side_copies:
        copy.wait_send()
    for copy in far_copies.values():
        copy.wait_send()


def scatter_sums(value_part, proj_part, table_part):
    group = lax.axis_size("dp")
    far = group // 4
    rows, width = value_part.shape[0] // group, value_part.shape[1]
    table_rows, lanes = table_part.shape[0], table_part.shape[1] // group
    tables = table_part.reshape(table_rows, group, lanes).transpose(1, 0, 2)
    tables = jnp.pad(tables, ((0, 0), (0, -table_rows % 8), (0, -lanes % 128)))
    count = 2 * far
    block = (rows, width)
    vmem = pl.BlockSpec(memory_space=pltpu.VMEM)
    dma = pltpu.SemaphoreType.DMA
    value_sum, proj_sum, table_sum = pl.pallas_call(
        functools.partial(scatter_kernel, far),
        out_shape=(
            jax.ShapeDtypeStruct(block, jnp.float32),
            jax.ShapeDtypeStruct((value_part.shape[0] // group, proj_part.shape[1]), jnp.float32),
            jax.ShapeDtypeStruct(tables.shape[1:], jnp.float32),
        ),
        in_specs=[vmem] * 3,
        out_specs=(vmem,) * 3,
        scratch_shapes=[
            pltpu.VMEM((2, count) + block, jnp.bfloat16),
            pltpu.VMEM((2,) + block, jnp.float32),
            pltpu.VMEM((count,) + block, jnp.bfloat16),
            pltpu.VMEM((count,) + block, jnp.bfloat16),
            pltpu.VMEM((count,) + block, jnp.bfloat16),
            pltpu.VMEM((count,) + block, jnp.bfloat16),
            pltpu.VMEM((group - 1,) + tables.shape[1:], jnp.float32),
            dma((2, count)), dma((2, count)), dma((count,)), dma((count,)),
            dma((count,)), dma((count,)), dma((group - 1,)), dma((group - 1,)),
        ],
        compiler_params=pltpu.CompilerParams(
            collective_id=0, has_side_effects=True, vmem_limit_bytes=56 * 1024 * 1024
        ),
    )(
        value_part.reshape((group,) + block),
        proj_part.reshape((group,) + block),
        tables,
    )
    return value_sum, proj_sum, table_sum[:table_rows, :lanes]


def modulation_rows(guide_bin, time_step, guide_table, section_row, tok_dev):
    group_size = lax.axis_size("dp")
    position = lax.axis_index("dp")
    batches, samples = guide_bin.shape
    rows_per = tok_dev * group_size // samples
    if rows_per % tok_dev == 0:
        owner = (position * tok_dev) // rows_per
        guide_bin = lax.dynamic_slice_in_dim(guide_bin, owner, 1, 1)
        time_step = lax.dynamic_slice_in_dim(time_step, owner, 1, 1)
    kept = guide_bin.shape[1]
    total = guide_table.shape[1]
    half = total // 2
    frequency = jnp.exp(-math.log(10000.0) * jnp.arange(half, dtype=jnp.float32) / half)
    angle = time_step.reshape(-1, 1).astype(jnp.float32) * frequency
    waves = jnp.concatenate([jnp.sin(angle), jnp.cos(angle)], axis=-1)
    bins = jnp.arange(guide_table.shape[0], dtype=jnp.int32)
    picked = jnp.sum(
        jnp.where(
            (guide_bin.reshape(-1, 1) == bins)[:, :, None], guide_table.astype(jnp.float32), 0.0
        ),
        axis=1,
    )
    rows = (picked + 0.5 * waves + section_row).reshape(batches, kept, total)
    if kept == samples and samples > 1:
        owners = (position * tok_dev + jnp.arange(tok_dev, dtype=jnp.int32)) // rows_per
        rows = jnp.take(rows, owners, axis=1)
    return rows


def blocks_kernel(x_ref, up_ref, mod_ref, wv_ref, wp_ref, mod_out, val_out, gv_out, gp_out,
                  tab_out, proj_s, gm_s, send_s, arrive_s, send_sem, recv_sem):
    units, rows, width = x_ref.shape
    depth = wv_ref.shape[1]
    chunk = math.gcd(rows, 16)
    section = lax.axis_index("section")
    barrier = pltpu.get_barrier_semaphore()
    pl.semaphore_signal(
        barrier, inc=1, device_id={"section": 1 - section}, device_id_type=MESH
    )
    pl.semaphore_wait(barrier, 1)
    tab_out[...] = jnp.zeros_like(tab_out)

    def hop(unit):
        return pltpu.make_async_remote_copy(
            src_ref=send_s.at[unit],
            dst_ref=arrive_s.at[unit],
            send_sem=send_sem.at[unit],
            recv_sem=recv_sem.at[unit],
            device_id={"section": 1 - section},
            device_id_type=MESH,
        )

    def each_chunk(body):
        @pl.loop(0, rows // chunk)
        def step(index):
            body(pl.ds(pl.multiple_of(index * chunk, chunk), chunk))

    def multiply(size, body):
        tile = math.gcd(size, 512)

        @pl.loop(0, size // tile)
        def step(index):
            body(pl.ds(pl.multiple_of(index * tile, tile), tile))

    def add_rows(place, value):
        tab_out[place] += jnp.sum(value.reshape(chunk // 8, 8, width), axis=0)

    def forward(unit, source, send):
        def modulate(part):
            normed, inverse = normalize(source[unit, part].astype(jnp.float32))
            scaled = normed * (1.0 + mod_ref[unit, 1:2]) + mod_ref[unit, 0:1]
            mod_out[unit, part] = scaled.astype(jnp.bfloat16)

        def first_dot(part):
            val_out[unit, :, part] = jnp.dot(
                mod_out[unit], wv_ref[:, part], preferred_element_type=jnp.float32
            ).astype(jnp.bfloat16)

        def second_dot(part):
            proj_s[unit, :, part] = jnp.dot(
                val_out[unit], wp_ref[:, part], preferred_element_type=jnp.float32
            )

        def add_gated(part):
            hidden = source[unit, part].astype(jnp.float32)
            block_out = hidden + mod_ref[unit, 2:3] * proj_s[unit, part]
            send_s[unit, part] = block_out.astype(jnp.bfloat16)

        each_chunk(modulate)
        multiply(depth, first_dot)
        multiply(width, second_dot)
        if send:
            each_chunk(add_gated)

    def backward(unit, source, upstream, send):
        def gated(part):
            grad_up = upstream[unit, part].astype(jnp.float32)
            gp_out[unit, part] = (mod_ref[unit, 2:3] * grad_up).astype(jnp.bfloat16)
            add_rows(2, grad_up * proj_s[unit, part])

        def first_dot(part):
            gv_out[unit, :, part] = lax.dot_general(
                gp_out[unit], wp_ref[part, :], (((1,), (1,)), ((), ())),
                preferred_element_type=jnp.float32,
            ).astype(jnp.bfloat16)

        def second_dot(part):
            gm_s[:, part] = lax.dot_general(
                gv_out[unit], wv_ref[part, :], (((1,), (1,)), ((), ())),
                preferred_element_type=jnp.float32,
            )

        def to_input(part):
            normed, inverse = normalize(source[unit, part].astype(jnp.float32))
            grad_mod = gm_s[part]
            add_rows(0, grad_mod)
            add_rows(1, grad_mod * normed)
            if send:
                grad_norm = grad_mod * (1.0 + mod_ref[unit, 1:2])
                centre_grad = jnp.mean(grad_norm, axis=-1, keepdims=True)
                cross = jnp.mean(grad_norm * normed, axis=-1, keepdims=True)
                grad_up = upstream[unit, part].astype(jnp.float32)
                grad_in = grad_up + inverse * (grad_norm - centre_grad - normed * cross)
                send_s[unit, part] = grad_in.astype(jnp.bfloat16)

        each_chunk(gated)
        multiply(depth, first_dot)
        multiply(width, second_dot)
        each_chunk(to_input)

    @pl.when(section == 0)
    def earlier():
        @pl.loop(0, units)
        def out(unit):
            forward(unit, x_ref, True)
            hop(unit).start()

        @pl.loop(0, units)
        def back(unit):
            hop(unit).wait_recv()
            backward(unit, x_ref, arrive_s, False)

    @pl.when(section == 1)
    def later():
        @pl.loop(0, units)
        def both(unit):
            hop(unit).wait_recv()
            forward(unit, arrive_s, False)
            backward(unit, arrive_s, up_ref, True)
            hop(unit).start()

    @pl.loop(0, units)
    def finish(unit):
        hop(unit).wait_send()


def per_device(
    inputs, out_grad, guide_bin, time_step, guide_table, section_table, value_weight, proj_weight
):
    units, rows, width = inputs.shape
    depth = value_weight.shape[2]
    group = lax.axis_size("dp")
    per_sample = rows * group // guide_bin.shape[1]
    if lax.axis_size("section") != 2 or group % 4 or per_sample % rows or rows % 8:
        return per_device_scan(
            inputs, out_grad, guide_bin, time_step, guide_table, section_table,
            value_weight, proj_weight,
        )
    modulation = modulation_rows(
        guide_bin, time_step, guide_table, section_table[0].reshape(-1), rows
    ).reshape(units, 3, width)
    vmem = pl.BlockSpec(memory_space=pltpu.VMEM)
    wide = jax.ShapeDtypeStruct((units, rows, width), jnp.bfloat16)
    deep = jax.ShapeDtypeStruct((units, rows, depth), jnp.bfloat16)
    modulated, values, grad_values, grad_proj, tables = pl.pallas_call(
        blocks_kernel,
        out_shape=(wide, deep, deep, wide, jax.ShapeDtypeStruct((3, 8, width), jnp.float32)),
        in_specs=[vmem] * 5,
        out_specs=(vmem,) * 5,
        scratch_shapes=[
            pltpu.VMEM((units, rows, width), jnp.float32),
            pltpu.VMEM((rows, width), jnp.float32),
            pltpu.VMEM((units, rows, width), jnp.bfloat16),
            pltpu.VMEM((units, rows, width), jnp.bfloat16),
            pltpu.SemaphoreType.DMA((units,)),
            pltpu.SemaphoreType.DMA((units,)),
        ],
        compiler_params=pltpu.CompilerParams(
            collective_id=1, has_side_effects=True, vmem_limit_bytes=56 * 1024 * 1024
        ),
    )(inputs, out_grad, modulation, value_weight[0], proj_weight[0])
    count = units * rows
    value_part = contract_rows(
        modulated.reshape(count, width), grad_values.reshape(count, depth)
    ).astype(jnp.bfloat16)
    proj_part = contract_rows(
        values.reshape(count, depth), grad_proj.reshape(count, width)
    ).astype(jnp.bfloat16)
    value_sum, proj_sum, table_sum = scatter_sums(value_part, proj_part, jnp.sum(tables, axis=1))
    return (value_sum[None], proj_sum[None], table_sum[None])


def solution(mesh):
    return jax.shard_map(
        per_device,
        mesh=mesh,
        in_specs=(
            P(None, "dp", None),
            P(None, "dp", None),
            P(),
            P(),
            P(),
            P("section", None, None),
            P("section", None, None),
            P("section", None, None),
        ),
        out_specs=(P("section", "dp", None), P("section", "dp", None), P("section", None, "dp")),
        check_vma=False,
    )
```

profile of v0, /device:TPU:0, one launch (start us, length us, event | category | flops | bytes accessed | tf_op | source)
XLA Modules:
  0.0 173.7 jit_solution(13906735988259335692)
XLA Ops:
  0.6 0.7 iota_compare_fusion
  1.4 0.7 convert_bitcast_fusion
  2.0 0.7 copy.31
  2.8 0.3 multiply_sine_fusion
  3.1 1.0 convert_element_type.14
  4.1 0.4 select_reduce_fusion
  4.5 0.7 copy_add_fusion.mod_ref
  5.2 80.2 %shard_map.106 = (bf16[4,128,1536]{2,1,0:T(8,128)(2,1)}, bf16[4,128,1536]{2,1,0:T(8,128)(2,1)}, bf16[4,128,1536]{2,1,0:T(8,128)(2,1)}, bf16[4,128,1536]{2,1,0:T(8,128)(2,1)}, f32[3,8,1536]{2,1,0:T(8,128)}) custom-call(bf16[4,128,1536]{2,1,0:T(8,128)(2,1)} %x_ref.1, bf16[4,128,1536]{2,1,0:T(8,128)(2,1)} %up_ref.1, f32[4,3,1536]{2,1,0:T(4,128)} %copy_add_fusion.mod_ref, ...), custom_call_target="tpu_custom_call" | custom-call | tf_op jit(solution)/shard_map/pallas_call | solution.py:556
  85.4 1.0 reduce_sum.19
  86.3 0.1 reshape.59
  86.4 0.6 pad.4.table_ref
  87.1 0.0 copy-start.1
  87.1 0.0 copy-start.2
  87.1 6.8 %bitcast_convert_fusion.1 = bf16[1536,1536]{1,0:T(8,128)(2,1)} fusion(bf16[4,128,1536]{2,1,0:T(8,128)(2,1)} %get-tuple-element.11, bf16[4,128,1536]{2,1,0:T(8,128)(2,1)} %get-tuple-element.12), kind=kOutput, calls=%fused_computation.1 | convolution fusion | flops 2418278400 | bytes 7864320 | tf_op jit(solution)/shard_map/dot_general | solution.py:43
  93.9 0.0 copy-done.1
  93.9 0.0 copy-done.2
  93.9 4.4 %bitcast_convert_fusion = bf16[1536,1536]{1,0:T(8,128)(2,1)} fusion(bf16[4,128,1536]{2,1,0:T(8,128)(2,1)S(1)} %copy-done.1, bf16[4,128,1536]{2,1,0:T(8,128)(2,1)S(1)} %copy-done.2), kind=kOutput, calls=%fused_computation | convolution fusion | flops 2418278400 | bytes 7864320 | tf_op jit(solution)/shard_map/dot_general | solution.py:43
  98.2 71.4 %shard_map.107 = (f32[96,1536]{1,0:T(8,128)}, f32[96,1536]{1,0:T(8,128)}, f32[8,128]{1,0:T(8,128)}) custom-call(bf16[16,96,1536]{2,1,0:T(8,128)(2,1)} %bitcast.28, bf16[16,96,1536]{2,1,0:T(8,128)(2,1)} %bitcast.29, f32[16,8,128]{2,1,0:T(8,128)} %pad.4.table_ref), custom_call_target="tpu_custom_call" | custom-call | tf_op jit(solution)/shard_map/pallas_call | solution.py:351
  169.6 0.0 copy-start
  169.6 0.7 slice_bitcast_fusion
  170.4 0.6 copy.23
  170.9 1.9 %copy.34 = f32[1,96,1536]{2,1,0:T(8,128)} copy(f32[1,96,1536]{2,1,0:T(8,128)} %bitcast.31) | data formatting | bytes 1179648
  172.9 0.0 copy-done
  172.9 0.8 copy.35
  (3 shorter events, 0.1 us)
Async XLA Ops:
  87.1 6.8 %copy-start.1 = (bf16[4,128,1536]{2,1,0:T(8,128)(2,1)S(1)}, bf16[4,128,1536]{2,1,0:T(8,128)(2,1)}, u32[]{:S(2)}) copy-start(bf16[4,128,1536]{2,1,0:T(8,128)(2,1)} %get-tuple-element.13) | copy-start | bytes 4718596
  87.1 6.8 %copy-start.2 = (bf16[4,128,1536]{2,1,0:T(8,128)(2,1)S(1)}, bf16[4,128,1536]{2,1,0:T(8,128)(2,1)}, u32[]{:S(2)}) copy-start(bf16[4,128,1536]{2,1,0:T(8,128)(2,1)} %get-tuple-element.14) | copy-start | bytes 4718596
  169.6 3.2 %copy-start = (f32[96,1536]{1,0:T(8,128)S(1)}, f32[96,1536]{1,0:T(8,128)}, u32[]{:S(2)}) copy-start(f32[96,1536]{1,0:T(8,128)} %get-tuple-element.17) | copy-start | bytes 1769476
where the time goes:
time: 174 us
  Pallas kernels  152 us (87%)
  matrix products  11.2 us (6%)
  local copies, waits for them, and re-layouts  5.52 us (3%)
  other arithmetic  4.77 us (3%)
    pallas_call x1, Pallas kernels, per_device(): pl.pallas_call(blocks_kernel, out_shape=(wide, deep, deep, wide, jax.Shap...  80.2 us
    pallas_call x1, Pallas kernels, scatter_sums(): pl.pallas_call(functools.partial(scatter_kernel, far), out_shape=(jax.Sha...  71.4 us
    dot_general x2, matrix products, contract_rows(): lax.dot_general(left, right, (((0,), (0,)), ((), ())), preferred_element_...  11.2 us
    unnamed x10, local copies, waits for them, and re-layouts  4.04 us

commit v1 on v0

--- a/solution.py
+++ b/solution.py
@@ -412,7 +412,7 @@
                   tab_out, proj_s, gm_s, send_s, arrive_s, send_sem, recv_sem):
     units, rows, width = x_ref.shape
     depth = wv_ref.shape[1]
-    chunk = math.gcd(rows, 16)
+    chunk = math.gcd(rows, 32)
     section = lax.axis_index("section")
     barrier = pltpu.get_barrier_semaphore()
     pl.semaphore_signal(

time: 174 us -> 165 us (0.948)
  Pallas kernels: 152 us -> 143 us
    pallas_call x1, Pallas kernels: 80.2 us -> 71.4 us  [per_device(): pl.pallas_call(blocks_kernel, out_shape=(wide, deep, deep, wide, jax.Shap...]
where the time goes in v1:
time: 165 us
  Pallas kernels  143 us (87%)
  matrix products  11.2 us (7%)
  local copies, waits for them, and re-layouts  5.52 us (3%)
  other arithmetic  4.77 us (3%)
    pallas_call x1, Pallas kernels, scatter_sums(): pl.pallas_call(functools.partial(scatter_kernel, far), out_shape=(jax.Sha...  71.4 us
    pallas_call x1, Pallas kernels, per_device(): pl.pallas_call(blocks_kernel, out_shape=(wide, deep, deep, wide, jax.Shap...  71.4 us
    dot_general x2, matrix products, contract_rows(): lax.dot_general(left, right, (((0,), (0,)), ((), ())), preferred_element_...  11.2 us
    unnamed x10, local copies, waits for them, and re-layouts  4.04 us

profile of v1, /device:TPU:0, one launch (start us, length us, event | category | flops | bytes accessed | tf_op | source)
XLA Modules:
  0.0 164.9 jit_solution(9435571365589547592)
XLA Ops:
  0.6 0.7 iota_compare_fusion
  1.4 0.7 convert_bitcast_fusion
  2.0 0.7 copy.31
  2.8 0.3 multiply_sine_fusion
  3.1 1.0 convert_element_type.14
  4.1 0.4 select_reduce_fusion
  4.5 0.7 copy_add_fusion.mod_ref
  5.2 71.4 %shard_map.106 = (bf16[4,128,1536]{2,1,0:T(8,128)(2,1)}, bf16[4,128,1536]{2,1,0:T(8,128)(2,1)}, bf16[4,128,1536]{2,1,0:T(8,128)(2,1)}, bf16[4,128,1536]{2,1,0:T(8,128)(2,1)}, f32[3,8,1536]{2,1,0:T(8,128)}) custom-call(bf16[4,128,1536]{2,1,0:T(8,128)(2,1)} %x_ref.1, bf16[4,128,1536]{2,1,0:T(8,128)(2,1)} %up_ref.1, f32[4,3,1536]{2,1,0:T(4,128)} %copy_add_fusion.mod_ref, ...), custom_call_target="tpu_custom_call" | custom-call | tf_op jit(solution)/shard_map/pallas_call | solution.py:556
  76.6 1.0 reduce_sum.19
  77.5 0.1 reshape.59
  77.6 0.6 pad.4.table_ref
  78.3 0.0 copy-start.1
  78.3 0.0 copy-start.2
  78.3 6.8 %bitcast_convert_fusion.1 = bf16[1536,1536]{1,0:T(8,128)(2,1)} fusion(bf16[4,128,1536]{2,1,0:T(8,128)(2,1)} %get-tuple-element.11, bf16[4,128,1536]{2,1,0:T(8,128)(2,1)} %get-tuple-element.12), kind=kOutput, calls=%fused_computation.1 | convolution fusion | flops 2418278400 | bytes 7864320 | tf_op jit(solution)/shard_map/dot_general | solution.py:43
  85.1 0.0 copy-done.1
  85.1 0.0 copy-done.2
  85.1 4.4 %bitcast_convert_fusion = bf16[1536,1536]{1,0:T(8,128)(2,1)} fusion(bf16[4,128,1536]{2,1,0:T(8,128)(2,1)S(1)} %copy-done.1, bf16[4,128,1536]{2,1,0:T(8,128)(2,1)S(1)} %copy-done.2), kind=kOutput, calls=%fused_computation | convolution fusion | flops 2418278400 | bytes 7864320 | tf_op jit(solution)/shard_map/dot_general | solution.py:43
  89.4 71.4 %shard_map.107 = (f32[96,1536]{1,0:T(8,128)}, f32[96,1536]{1,0:T(8,128)}, f32[8,128]{1,0:T(8,128)}) custom-call(bf16[16,96,1536]{2,1,0:T(8,128)(2,1)} %bitcast.28, bf16[16,96,1536]{2,1,0:T(8,128)(2,1)} %bitcast.29, f32[16,8,128]{2,1,0:T(8,128)} %pad.4.table_ref), custom_call_target="tpu_custom_call" | custom-call | tf_op jit(solution)/shard_map/pallas_call | solution.py:351
  160.8 0.0 copy-start
  160.8 0.7 slice_bitcast_fusion
  161.6 0.6 copy.23
  162.1 1.9 %copy.34 = f32[1,96,1536]{2,1,0:T(8,128)} copy(f32[1,96,1536]{2,1,0:T(8,128)} %bitcast.31) | data formatting | bytes 1179648
  164.0 0.0 copy-done
  164.0 0.8 copy.35
  (3 shorter events, 0.1 us)
Async XLA Ops:
  78.3 6.8 %copy-start.1 = (bf16[4,128,1536]{2,1,0:T(8,128)(2,1)S(1)}, bf16[4,128,1536]{2,1,0:T(8,128)(2,1)}, u32[]{:S(2)}) copy-start(bf16[4,128,1536]{2,1,0:T(8,128)(2,1)} %get-tuple-element.13) | copy-start | bytes 4718596
  78.3 6.8 %copy-start.2 = (bf16[4,128,1536]{2,1,0:T(8,128)(2,1)S(1)}, bf16[4,128,1536]{2,1,0:T(8,128)(2,1)}, u32[]{:S(2)}) copy-start(bf16[4,128,1536]{2,1,0:T(8,128)(2,1)} %get-tuple-element.14) | copy-start | bytes 4718596
  160.8 3.2 %copy-start = (f32[96,1536]{1,0:T(8,128)S(1)}, f32[96,1536]{1,0:T(8,128)}, u32[]{:S(2)}) copy-start(f32[96,1536]{1,0:T(8,128)} %get-tuple-element.17) | copy-start | bytes 1769476
